TPU v7x, 256 devices: a whole 4x4x8 slice. The times are simulated.
256 devices in a mesh: group: 8 (over z), shard: 32 (over x, y, core).
Axes of the slice: x: 4, y: 4, z: 8, core: 2. Of those that a mesh axis runs over, the one named last changes fastest.
Arguments:
- queries: bfloat16 [1536, 1024], P(('group', 'shard')), may hold values from -12 to 12
- candidates: bfloat16 [1048576, 1024], P(('group', 'shard')), may hold values from -4 to 4
- targets: int32 [1536], replicated, may hold values from 0 to 1048575
Outputs:
- losses: float32 [1536], replicated
- mean_loss: float32 [], replicated
All inputs are finite; a program needn't handle non-finite values.
Results may differ from a plain program's by a relative error of at most 0.0003.
Values may be sent and summed in bfloat16 or wider, within the bound.
A program may use at most 64 MiB of HBM per device.

v0:
```python
import math
import jax
import jax.numpy as jnp
from jax import lax
from jax.sharding import Mesh
from jax.sharding import PartitionSpec as P

SHARD = ("shard_0", "shard_1", "shard_2")
GROUP_SHARD = ("group", "shard_0", "shard_1", "shard_2")


def laid_out(tiles, dim):
    shape = list(tiles.shape[1:])
    shape[dim] *= tiles.shape[0]
    return jnp.moveaxis(tiles, 0, dim).reshape(shape)


def gather_in_order(value, axes, order):
    tiles = value[None]
    for k in order:
        tiles = lax.all_gather(tiles, axes[k], axis=0, tiled=True)
    held = [lax.axis_size(axes[k]) for k in reversed(order)]
    tiles = tiles.reshape(*held, *value.shape)
    turned = sorted(range(len(order)), key=lambda place: order[len(order) - 1 - place])
    return tiles.transpose(*turned, *range(len(order), tiles.ndim)).reshape(-1, *value.shape)


def gather_axes(value, axes, order, dim):
    return laid_out(gather_in_order(value, axes, order), dim)


def from_everyone(value, axis):
    copies = jnp.broadcast_to(value, (lax.axis_size(axis), *value.shape))
    return lax.all_to_all(copies, axis, split_axis=0, concat_axis=0, tiled=True)


def collected_together(value, axis):
    leaves = jax.tree.leaves(value)
    order = sorted(range(len(leaves)), key=lambda k: -leaves[k].size)
    width = (1, *leaves[order[0]].shape)[-1]
    lines = [
        jnp.pad(leaves[k].reshape(-1), (0, -leaves[k].size % width)).reshape(-1, width)
        for k in order
    ]
    both, at, found = (from_everyone(jnp.concatenate(lines), axis), 0, {})
    for k, line in zip(order, lines):
        share = both[:, at : at + len(line)].reshape(len(both), -1)
        found[k] = share[:, : leaves[k].size].reshape(-1, *leaves[k].shape)
        at += len(line)
    numbers = iter(range(len(leaves)))
    return jax.tree.map(lambda _: found[next(numbers)], value)


def folded_in_pairs(pieces, combine):
    while len(jax.tree.leaves(pieces)[0]) > 1:
        pieces = jax.vmap(combine)(
            *(jax.tree.map(lambda part: part[side::2], pieces) for side in (0, 1))
        )
    return jax.tree.map(lambda part: part[0], pieces)


def combined_all(value, axis, combine):
    pieces = collected_together(value, axis)
    return folded_in_pairs(pieces, combine)


def once_a_type(value, axis):
    leaves, found = (jax.tree.leaves(value), {})
    for leading, a in enumerate(leaves):
        if leading not in found:
            alike = [k for k, b in enumerate(leaves) if b.dtype == a.dtype]
            got = (
                collected_together([leaves[k] for k in alike], axis)
                if len(alike) > 1
                else [from_everyone(a, axis)]
            )
            for k, b in zip(alike, got):
                found[k] = b
    numbers = iter(range(len(leaves)))
    return jax.tree.map(lambda _: found[next(numbers)], value)


def merged(value, axis, combine):
    pieces = once_a_type(value, axis)
    return folded_in_pairs(pieces, combine)


def combine(first, second):
    top = jnp.maximum(first[0], second[0])
    total = first[1] * jnp.exp(first[0] - top) + second[1] * jnp.exp(second[0] - top)
    return (top, total, first[2] + second[2])


def score_rows(piece, candidates, chosen_targets, owner):
    rows = candidates.shape[0]
    local = chosen_targets - owner * rows
    owned = (local >= 0) & (local < rows)
    chosen = jnp.take(candidates, jnp.clip(local, 0, rows - 1), axis=0)
    products = jnp.sum(piece.astype(jnp.float32) * chosen.astype(jnp.float32), axis=1)
    picked = jnp.where(owned, products, jnp.float32(0.0))
    count = piece.shape[0]
    block = math.gcd(count, 512)
    panels = piece.reshape(count // block, block, piece.shape[1])

    def score_panel(panel):
        scores = jnp.dot(panel, candidates.T, preferred_element_type=jnp.float32)
        peak = jnp.max(scores, axis=1)
        return (peak, jnp.sum(jnp.exp(scores - peak[:, None]), axis=1))

    peaks, sums = lax.map(score_panel, panels)
    return (peaks.reshape(count), sums.reshape(count), picked)


def on_device(queries, candidates, targets):
    owner = lax.axis_index("group") * lax.axis_size(SHARD) + lax.axis_index(SHARD)
    every = gather_axes(queries, GROUP_SHARD, (1, 0, 2, 3), 0)
    top, total, picked = score_rows(every, candidates, targets, owner)
    inner = combined_all((top, total, picked), SHARD, combine)
    top, total, picked = merged(inner, "group", combine)
    losses = top + jnp.log(total) - picked
    return (losses, jnp.mean(losses))


def solution(mesh):
    finer = Mesh(
        mesh.devices.reshape(mesh.shape["group"], 4, 4, 2),
        ("group", "shard_0", "shard_1", "shard_2"),
    )
    in_specs = (P(GROUP_SHARD, None), P(GROUP_SHARD, None), P())
    out_specs = (P(), P())
    return jax.shard_map(
        on_device, mesh=finer, in_specs=in_specs, out_specs=out_specs, check_vma=False
    )
```

profile of v0, /device:TPU:1, one launch (start us, length us, event | category | flops | bytes accessed | tf_op | source)
XLA Modules:
  0.0 195.4 jit_solution(15849809175005774843)
XLA Ops:
  7.2 0.0 all-gather.5.cloned.1.call-start
  7.2 10.4 %all-gather.1 = bf16[4,6,1024]{2,1,0:T(8,128)(2,1)S(1)} all-gather(bf16[1,6,1024]{2,1,0:T(8,128)(2,1)} %bitcast.56), channel_id=2, replica_groups=mesh['group'=8,'shard_0'=4,'shard_1'=4,'shard_2'=2] {'shard_0'}, dimensions={0}, use_global_device_ids=true | all-gather | bytes 61440 | tf_op jit(solution)/shard_map/all_gather | solution.py:21
  17.6 23.3 %all_gather.13 = bf16[32,6,1024]{2,1,0:T(8,128)(2,1)S(1)} all-gather(bf16[4,6,1024]{2,1,0:T(8,128)(2,1)S(1)} %all-gather.1), channel_id=1, replica_groups=mesh['group'=8,'shard_0'=4,'shard_1'=4,'shard_2'=2] {'group'}, dimensions={0}, use_global_device_ids=true | all-gather | bytes 442368 | tf_op jit(solution)/shard_map/all_gather | solution.py:21
  40.9 1.0 copy.36
  41.8 0.0 all-gather.5.cloned.1.call-update
  41.9 0.0 all-gather.7.cloned.1.call-start
  41.9 36.5 %all-gather.5.cloned.1.call-done = bf16[128,6,1024]{2,0,1:T(8,128)(2,1)} async-done(((bf16[32,6,1024]{2,0,1:T(8,128)(2,1)}), bf16[128,6,1024]{2,0,1:T(8,128)(2,1)}) %all-gather.5.cloned.1.call-update) | async-done | bytes 1572880 | tf_op jit(solution)/shard_map/all_gather | solution.py:21
  78.4 0.0 all-gather.7.cloned.1.call-update
  78.5 0.7 compare_and_fusion
  79.2 11.6 %gather_fusion = bf16[1536,1024]{1,0:T(8,128)(2,1)S(1)} fusion(bf16[4096,1024]{1,0:T(8,128)(2,1)} %param.6, s32[2048]{0:T(1024)S(1)} %pad_clamp_fusion), kind=kCustom, calls=%fused_computation | custom fusion | bytes 6297600 | tf_op jit(solution)/shard_map/jit(_take)/gather | solution.py:98
  90.8 2.9 %gather.7 = bf16[8,4,4,2,6,1024]{5,4,3,2,1,0:T(8,128)(2,1)} reshape(bf16[1536,1024]{1,0:T(8,128)(2,1)S(1)} %gather_fusion) | data formatting | bytes 6291456 | tf_op jit(solution)/shard_map/jit(_take)/gather | solution.py:98
  93.7 0.2 broadcast_in_dim.36
  93.9 0.6 copy.38
  94.5 4.1 %all-gather.7.cloned.1.call-done = bf16[256,6,1024]{2,0,1:T(8,128)(2,1)} async-done(((bf16[128,6,1024]{2,0,1:T(8,128)(2,1)}), bf16[256,6,1024]{2,0,1:T(8,128)(2,1)}) %all-gather.7.cloned.1.call-update) | async-done | bytes 3145744 | tf_op jit(solution)/shard_map/all_gather | solution.py:21
  98.6 4.0 %reshape.57 = bf16[2,4,8,4,6,1024]{5,3,2,1,0,4:T(4,128)(2,1)S(1)} reshape(bf16[256,6,1024]{2,0,1:T(8,128)(2,1)} %all-gather.7.cloned.1.call-done) | data formatting | bytes 6291456 | tf_op jit(solution)/shard_map/reshape | solution.py:23
  102.6 0.0 copy-start
  102.6 7.8 %multiply_reduce_fusion = f32[8,4,4,2,6]{1,0,2,3,4:T(8,128)S(1)} fusion(bf16[8,4,4,2,6,1024]{5,4,3,2,1,0:T(8,128)(2,1)} %gather.7, pred[8,4,4,2,6]{1,0,2,3,4:T(8,128)(4,1)S(1)} %copy.38, bf16[2,4,8,4,6,1024]{5,3,2,1,0,4:T(4,128)(2,1)S(1)} %reshape.57), kind=kLoop, calls=%fused_computation.6 | loop fusion | flops 7862784 | bytes 6299136 | tf_op jit(solution)/shard_map/reduce_sum | solution.py:99
  110.4 0.5 copy.40
  111.0 0.2 reduce_sum.30
  111.2 0.0 copy-done
  111.2 3.7 %copy.37 = bf16[8,4,4,2,6,1024]{5,4,3,2,1,0:T(8,128)(2,1)} copy(bf16[8,4,4,2,6,1024]{5,1,0,2,3,4:T(4,128)(2,1)S(1)} %bitcast.43) | data formatting | bytes 6291456 | tf_op jit(solution)/shard_map/transpose | solution.py:25
  115.0 4.9 %reshape_reshape_reshape.3 = bf16[3,512,1024]{2,1,0:T(8,128)(2,1)S(1)} reshape(bf16[8,4,4,2,6,1024]{5,4,3,2,1,0:T(8,128)(2,1)} %copy.37) | data formatting | bytes 6291456 | tf_op jit(solution)/shard_map/reshape;reshape;reshape | solution.py:103
  119.8 25.6 %while.12 = (s32[]{:T(128)}, f32[3,512]{1,0:T(4,128)S(1)}, f32[3,512]{1,0:T(4,128)S(1)}, bf16[3,512,1024]{2,1,0:T(8,128)(2,1)S(1)}, bf16[4096,1024]{1,0:T(8,128)(2,1)}, /*index=5*/s32[]{:T(128)}, s32[]{:T(128)}) while((s32[]{:T(128)}, f32[3,512]{1,0:T(4,128)S(1)}, f32[3,512]{1,0:T(4,128)S(1)}, bf16[3,512,1024]{2,1,0:T(8,128)(2,1)S(1)}, ...), condition=%wide.region_3.4_spmd, body=%wide.region_0.0_spmd.sunk | while | flops 4301257728 | bytes 26228824 | solution.py:110
  119.9 7.1 %fusion.16 = (f32[512]{0:T(512)S(1)}, f32[512,4096]{1,0:T(8,128)S(1)}) fusion(bf16[4096,1024]{1,0:T(8,128)(2,1)} %get-tuple-element.123, bf16[3,512,1024]{2,1,0:T(8,128)(2,1)S(1)} %get-tuple-element.122, s32[]{:T(128)} %get-tuple-element.112), kind=kOutput, calls=%fused_computation.39.clone.1 | convolution fusion | flops 4297063936 | bytes 17827844 | tf_op jit(solution)/shard_map/while/body/eval_jaxpr/dot_general | solution.py:106
  127.0 1.3 exponential_reduce_fusion.2
  128.3 0.1 dynamic_update_slice.9
  128.4 7.1 %fusion.16 = (f32[512]{0:T(512)S(1)}, f32[512,4096]{1,0:T(8,128)S(1)}) fusion(bf16[4096,1024]{1,0:T(8,128)(2,1)} %get-tuple-element.123, bf16[3,512,1024]{2,1,0:T(8,128)(2,1)S(1)} %get-tuple-element.122, s32[]{:T(128)} %get-tuple-element.112), kind=kOutput, calls=%fused_computation.39.clone.1 | convolution fusion | flops 4297063936 | bytes 17827844 | tf_op jit(solution)/shard_map/while/body/eval_jaxpr/dot_general | solution.py:106
  135.5 1.3 exponential_reduce_fusion.2
  136.8 0.1 dynamic_update_slice.9
  136.9 7.1 %fusion.16 = (f32[512]{0:T(512)S(1)}, f32[512,4096]{1,0:T(8,128)S(1)}) fusion(bf16[4096,1024]{1,0:T(8,128)(2,1)} %get-tuple-element.123, bf16[3,512,1024]{2,1,0:T(8,128)(2,1)S(1)} %get-tuple-element.122, s32[]{:T(128)} %get-tuple-element.112), kind=kOutput, calls=%fused_computation.39.clone.1 | convolution fusion | flops 4297063936 | bytes 17827844 | tf_op jit(solution)/shard_map/while/body/eval_jaxpr/dot_general | solution.py:106
  144.0 1.3 exponential_reduce_fusion.2
  145.4 0.1 dynamic_update_slice.9
  145.5 0.1 broadcast_in_dim.41
  145.6 20.8 %all_to_all.10 = f32[32,3,1536]{2,1,0:T(4,128)S(1)} all-to-all(f32[32,3,1536]{2,1,0:T(4,128)S(1)} %broadcast_in_dim.41), channel_id=1, replica_groups=mesh['group'=8,'shard_0'=4,'shard_1'=4,'shard_2'=2] {'shard_0','shard_1'..., dimensions={0} | all-to-all | bytes 1179648 | tf_op jit(solution)/shard_map/all_to_all | solution.py:34
  166.5 0.4 fusion.10
  168.0 17.4 %all_to_all.11 = f32[8,3,1536]{2,1,0:T(4,128)S(1)} all-to-all(f32[8,3,1536]{2,1,0:T(4,128)S(1)} %broadcast_in_dim.42), channel_id=1, replica_groups=mesh['group'=8,'shard_0'=4,'shard_1'=4,'shard_2'=2] {'group'}, dimensions={0} | all-to-all | bytes 294912 | tf_op jit(solution)/shard_map/all_to_all | solution.py:34
  185.5 0.1 fusion.11
  186.0 0.7 fusion.8
  (68 shorter events, 1.6 us)
Async XLA Ops:
  7.2 71.3 %all-gather.5.cloned.1.call-start = ((), (), s32[]{:S(2)}) async-start(), calls=%async_computation.2 | async-start | bytes 1966080 | tf_op jit(solution)/shard_map/all_gather | solution.py:21
  41.9 56.7 %all-gather.7.cloned.1.call-start = ((), (), s32[]{:S(2)}) async-start(), calls=%async_computation.3 | async-start | bytes 4718592 | tf_op jit(solution)/shard_map/all_gather | solution.py:21
  102.6 8.6 %copy-start = (s32[1536]{0:T(1024)S(1)}, s32[1536]{0:T(1024)}, u32[]{:S(2)}) copy-start(s32[1536]{0:T(1024)} %param.7) | copy-start | bytes 18436
Sparse Core Ops, SparseCore 0:
  42.0 36.4 all-gather.4
  80.2 18.3 all-gather.6
where the time goes:
time: 196 us; the launch traced here: 195 us
  blocking collectives  71.9 us (37%)
  waiting for transfers between devices  40.6 us (21%)
  local copies, waits for them, and re-layouts  31.7 us (16%)
  matrix products  21.4 us (11%)
  between operations  16.2 us (8%)
  other arithmetic  13.4 us (7%)
    all_gather x2, waiting for transfers between devices, gather_in_order(): tiles = lax.all_gather(tiles, axes[k], axis=0, tiled=True)  40.6 us
    all_to_all x2, blocking collectives, from_everyone(): return lax.all_to_all(copies, axis, split_axis=0, concat_axis=0, tiled=True)  38.3 us
    all_gather x2, blocking collectives, gather_in_order(): tiles = lax.all_gather(tiles, axes[k], axis=0, tiled=True)  33.7 us
    dot_general x3, matrix products, score_panel(): scores = jnp.dot(panel, candidates.T, preferred_element_type=jnp.float32)  21.4 us
    gather x2, local copies, waits for them, and re-layouts, score_rows(): chosen = jnp.take(candidates, jnp.clip(local, 0, rows - 1), axis=0)  14.5 us
    reduce_sum x1, other arithmetic, score_rows(): jnp.sum(piece.astype(jnp.float32) * chosen.astype(jnp.float32), axis=1)  7.8 us
    another operation x1, local copies, waits for them, and re-layouts, score_rows(): panels = piece.reshape(count // block, block, piece.shape[1])  4.87 us
    reshape x1, local copies, waits for them, and re-layouts, gather_in_order(): tiles = tiles.reshape(*held, *value.shape)  4.01 us
  transfers between devices with their start and end apart: 2, of which 2 were waited for; matrix products, arithmetic and copies ran while one was open for 8% of the time, Pallas kernels for 0%

commit v1 on v0

--- a/solution.py
+++ b/solution.py
@@ -18,7 +18,9 @@
 def gather_in_order(value, axes, order):
     tiles = value[None]
     for k in order:
-        tiles = lax.all_gather(tiles, axes[k], axis=0, tiled=True)
+        tiles = jnp.concatenate(
+            lax.all_to_all(jnp.stack([tiles] * lax.axis_size(axes[k])), axes[k], 0, 0), axis=0
+        )
     held = [lax.axis_size(axes[k]) for k in reversed(order)]
     tiles = tiles.reshape(*held, *value.shape)
     turned = sorted(range(len(order)), key=lambda place: order[len(order) - 1 - place])

time: 196 us -> 149 us (0.76)
  waiting for transfers between devices: 40.6 us -> 0.79 us
  between operations: 16.2 us -> 2.85 us
  starting transfers between devices: 0.08 us -> 4.35 us
  local copies, waits for them, and re-layouts: 31.7 us -> 34.2 us
    all_gather x2 -> x0, waiting for transfers between devices: 40.6 us -> none  [gather_in_order(): tiles = lax.all_gather(tiles, axes[k], axis=0, tiled=True)]
    all_to_all x0 -> x3, blocking collectives: none -> 40 us  [gather_in_order(): lax.all_to_all(jnp.stack([tiles] * lax.axis_size(axes[k])), axes[k], 0, 0)]
    all_gather x2 -> x0, blocking collectives: 33.7 us -> none  [gather_in_order(): tiles = lax.all_gather(tiles, axes[k], axis=0, tiled=True)]
    all_to_all x2, blocking collectives: 38.3 us -> 32.5 us  [from_everyone(): return lax.all_to_all(copies, axis, split_axis=0, concat_axis=0, tiled=True)]
    all_to_all x0 -> x3, local copies, waits for them, and re-layouts: none -> 4.97 us  [gather_in_order(): lax.all_to_all(jnp.stack([tiles] * lax.axis_size(axes[k])), axes[k], 0, 0)]
    all_to_all x0 -> x1, starting transfers between devices: none -> 4.35 us  [gather_in_order(): lax.all_to_all(jnp.stack([tiles] * lax.axis_size(axes[k])), axes[k], 0, 0)]
    reshape x1 -> x0, local copies, waits for them, and re-layouts: 4.01 us -> none  [gather_in_order(): tiles = tiles.reshape(*held, *value.shape)]
    another operation x0 -> x5, local copies, waits for them, and re-layouts: none -> 2.37 us  [gather_in_order(): jnp.stack([tiles] * lax.axis_size(axes[k]))]
  transfers between devices with their start and end apart: 2 -> 1, of which waited for: 2 -> 1; matrix products, arithmetic and copies ran while one was open for 8% -> 10% of each run, Pallas kernels for 0% -> 0%
where the time goes in v1:
time: 149 us
  blocking collectives  72.5 us (49%)
  local copies, waits for them, and re-layouts  34.2 us (23%)
  matrix products  21.4 us (14%)
  other arithmetic  12.7 us (9%)
  starting transfers between devices  4.35 us (3%)
  between operations  2.85 us (2%)
    all_to_all x3, blocking collectives, gather_in_order(): lax.all_to_all(jnp.stack([tiles] * lax.axis_size(axes[k])), axes[k], 0, 0)  40 us
    all_to_all x2, blocking collectives, from_everyone(): return lax.all_to_all(copies, axis, split_axis=0, concat_axis=0, tiled=True)  32.5 us
    dot_general x3, matrix products, score_panel(): scores = jnp.dot(panel, candidates.T, preferred_element_type=jnp.float32)  21.4 us
    gather x2, local copies, waits for them, and re-layouts, score_rows(): chosen = jnp.take(candidates, jnp.clip(local, 0, rows - 1), axis=0)  14.4 us
    reduce_sum x1, other arithmetic, score_rows(): jnp.sum(piece.astype(jnp.float32) * chosen.astype(jnp.float32), axis=1)  7.52 us
    all_to_all x3, local copies, waits for them, and re-layouts, gather_in_order(): lax.all_to_all(jnp.stack([tiles] * lax.axis_size(axes[k])), axes[k], 0, 0)  4.97 us
    another operation x1, local copies, waits for them, and re-layouts, score_rows(): panels = piece.reshape(count // block, block, piece.shape[1])  4.88 us
    all_to_all x1, starting transfers between devices, gather_in_order(): lax.all_to_all(jnp.stack([tiles] * lax.axis_size(axes[k])), axes[k], 0, 0)  4.35 us
  transfers between devices with their start and end apart: 1, of which 1 were waited for; matrix products, arithmetic and copies ran while one was open for 10% of the time, Pallas kernels for 0%

profile of v1, /device:TPU:1, one launch (start us, length us, event | category | flops | bytes accessed | tf_op | source)
XLA Modules:
  0.0 148.8 jit_solution(5390928843071028787)
XLA Ops:
  0.6 0.7 stack.12
  1.4 9.1 %all_to_all.30 = bf16[4,1,6,1024]{3,2,1,0:T(8,128)(2,1)S(1)} all-to-all(bf16[4,1,6,1024]{3,2,1,0:T(8,128)(2,1)S(1)} %stack.12), channel_id=1, replica_groups=mesh['group'=8,'shard_0'=4,'shard_1'=4,'shard_2'=2] {'shard_0'}, dimensions={0} | all-to-all | bytes 98304 | tf_op jit(solution)/shard_map/all_to_all | solution.py:22
  10.5 0.1 stack.13
  10.6 19.6 %all_to_all.31 = bf16[8,4,6,1024]{3,1,2,0:T(4,128)(2,1)S(1)} all-to-all(bf16[8,4,6,1024]{3,1,2,0:T(4,128)(2,1)S(1)} %stack.13), channel_id=1, replica_groups=mesh['group'=8,'shard_0'=4,'shard_1'=4,'shard_2'=2] {'group'}, dimensions={0} | all-to-all | bytes 786432 | tf_op jit(solution)/shard_map/all_to_all | solution.py:22
  30.2 0.1 copy.56
  30.4 0.0 copy-start.1
  30.4 0.1 stack_reshape.7
  30.5 1.4 stack.14
  31.8 4.3 %all-to-all-start.2 = ((bf16[4,32,6,1024]{3,1,2,0:T(8,128)(2,1)}), bf16[4,32,6,1024]{3,1,2,0:T(8,128)(2,1)}, u32[]{:S(2)}, u32[]{:S(2)}) async-start(bf16[4,32,6,1024]{3,1,2,0:T(8,128)(2,1)} %stack.14), calls=%async_computation.2 | async-start | bytes 3145728 | tf_op jit(solution)/shard_map/all_to_all | solution.py:22
  36.2 0.0 copy-done.1
  36.3 11.6 %gather_fusion = bf16[1536,1024]{1,0:T(8,128)(2,1)S(1)} fusion(bf16[4096,1024]{1,0:T(8,128)(2,1)} %param.6, s32[2048]{0:T(1024)S(1)} %pad_clamp_fusion), kind=kCustom, calls=%fused_computation | custom fusion | bytes 6297600 | tf_op jit(solution)/shard_map/jit(_take)/gather | solution.py:100
  47.8 2.9 %gather.7 = bf16[8,4,4,2,6,1024]{5,4,3,2,1,0:T(8,128)(2,1)} reshape(bf16[1536,1024]{1,0:T(8,128)(2,1)S(1)} %gather_fusion) | data formatting | bytes 6291456 | tf_op jit(solution)/shard_map/jit(_take)/gather | solution.py:100
  50.7 0.2 broadcast_in_dim.32
  50.9 0.9 copy.60
  51.8 0.8 all-to-all-done.2
  52.6 1.6 %copy.57 = bf16[4,32,6,1024]{3,1,0,2:T(8,128)(2,1)S(1)} copy(bf16[4,32,6,1024]{3,1,2,0:T(8,128)(2,1)} %all-to-all-done.2) | data formatting | bytes 3145728 | tf_op jit(solution)/shard_map/all_to_all | solution.py:22
  54.2 0.3 pad_maximum_fusion
  54.5 11.3 %all_to_all.32 = bf16[2,128,6,1024]{3,1,2,0:T(8,128)(2,1)S(1)} all-to-all(bf16[2,128,6,1024]{3,1,2,0:T(8,128)(2,1)S(1)} %pad_maximum_fusion), channel_id=1, replica_groups=mesh['group'=8,'shard_0'=4,'shard_1'=4,'shard_2'=2] {'shard_2'}, dimensions={0} | all-to-all | bytes 6291456 | tf_op jit(solution)/shard_map/all_to_all | solution.py:22
  65.8 3.2 %copy.58 = bf16[2,128,6,1024]{3,0,2,1:T(2,128)(2,1)S(1)} copy(bf16[2,128,6,1024]{3,1,2,0:T(8,128)(2,1)S(1)} %all_to_all.32) | data formatting | bytes 6291456 | tf_op jit(solution)/shard_map/all_to_all | solution.py:22
  69.0 0.0 copy-start
  69.0 3.3 %copy.59 = bf16[8,4,4,2,6,1024]{5,4,3,2,1,0:T(8,128)(2,1)} copy(bf16[8,4,4,2,6,1024]{5,3,4,1,0,2:T(2,128)(2,1)S(1)} %bitcast.45) | data formatting | bytes 6291456 | tf_op jit(solution)/shard_map/transpose | solution.py:27
  72.3 0.0 copy-done
  72.3 7.5 %multiply_reduce_fusion = f32[8,4,4,2,6]{3,4,1,0,2:T(8,128)S(1)} fusion(bf16[8,4,4,2,6,1024]{5,3,4,1,0,2:T(2,128)(2,1)S(1)} %bitcast.46, pred[8,4,4,2,6]{3,4,1,0,2:T(8,128)(4,1)S(1)} %copy.60, bf16[8,4,4,2,6,1024]{5,4,3,2,1,0:T(8,128)(2,1)S(1)} %copy-done), kind=kLoop, calls=%fused_computation.6 | loop fusion | flops 7862784 | bytes 6299136 | tf_op jit(solution)/shard_map/reduce_sum | solution.py:101
  79.9 0.9 copy.62
  80.7 0.2 reduce_sum.30
  81.0 4.9 %reshape_reshape_reshape.3 = bf16[3,512,1024]{2,1,0:T(8,128)(2,1)S(1)} reshape(bf16[8,4,4,2,6,1024]{5,4,3,2,1,0:T(8,128)(2,1)} %copy.59) | data formatting | bytes 6291456 | tf_op jit(solution)/shard_map/reshape;reshape;reshape | solution.py:105
  85.9 25.6 %while.12 = (s32[]{:T(128)}, f32[3,512]{1,0:T(4,128)S(1)}, f32[3,512]{1,0:T(4,128)S(1)}, bf16[3,512,1024]{2,1,0:T(8,128)(2,1)S(1)}, bf16[4096,1024]{1,0:T(8,128)(2,1)}, /*index=5*/s32[]{:T(128)}, s32[]{:T(128)}) while((s32[]{:T(128)}, f32[3,512]{1,0:T(4,128)S(1)}, f32[3,512]{1,0:T(4,128)S(1)}, bf16[3,512,1024]{2,1,0:T(8,128)(2,1)S(1)}, ...), condition=%wide.region_3.4_spmd, body=%wide.region_0.0_spmd.sunk | while | flops 4301257728 | bytes 26228824 | solution.py:112
  85.9 7.1 %fusion.16 = (f32[512]{0:T(512)S(1)}, f32[512,4096]{1,0:T(8,128)S(1)}) fusion(bf16[4096,1024]{1,0:T(8,128)(2,1)} %get-tuple-element.123, bf16[3,512,1024]{2,1,0:T(8,128)(2,1)S(1)} %get-tuple-element.122, s32[]{:T(128)} %get-tuple-element.112), kind=kOutput, calls=%fused_computation.40.clone.1 | convolution fusion | flops 4297063936 | bytes 17827844 | tf_op jit(solution)/shard_map/while/body/eval_jaxpr/dot_general | solution.py:108
  93.0 1.3 exponential_reduce_fusion.2
  94.3 0.1 dynamic_update_slice.9
  94.4 7.1 %fusion.16 = (f32[512]{0:T(512)S(1)}, f32[512,4096]{1,0:T(8,128)S(1)}) fusion(bf16[4096,1024]{1,0:T(8,128)(2,1)} %get-tuple-element.123, bf16[3,512,1024]{2,1,0:T(8,128)(2,1)S(1)} %get-tuple-element.122, s32[]{:T(128)} %get-tuple-element.112), kind=kOutput, calls=%fused_computation.40.clone.1 | convolution fusion | flops 4297063936 | bytes 17827844 | tf_op jit(solution)/shard_map/while/body/eval_jaxpr/dot_general | solution.py:108
  101.5 1.3 exponential_reduce_fusion.2
  102.9 0.1 dynamic_update_slice.9
  102.9 7.1 %fusion.16 = (f32[512]{0:T(512)S(1)}, f32[512,4096]{1,0:T(8,128)S(1)}) fusion(bf16[4096,1024]{1,0:T(8,128)(2,1)} %get-tuple-element.123, bf16[3,512,1024]{2,1,0:T(8,128)(2,1)S(1)} %get-tuple-element.122, s32[]{:T(128)} %get-tuple-element.112), kind=kOutput, calls=%fused_computation.40.clone.1 | convolution fusion | flops 4297063936 | bytes 17827844 | tf_op jit(solution)/shard_map/while/body/eval_jaxpr/dot_general | solution.py:108
  110.1 1.3 exponential_reduce_fusion.2
  111.4 0.1 dynamic_update_slice.9
  111.5 0.1 broadcast_in_dim.37
  111.6 18.0 %all_to_all.33 = f32[32,3,1536]{2,1,0:T(4,128)S(1)} all-to-all(f32[32,3,1536]{2,1,0:T(4,128)S(1)} %broadcast_in_dim.37), channel_id=1, replica_groups=mesh['group'=8,'shard_0'=4,'shard_1'=4,'shard_2'=2] {'shard_0','shard_1'..., dimensions={0} | all-to-all | bytes 1179648 | tf_op jit(solution)/shard_map/all_to_all | solution.py:36
  129.6 0.4 fusion.10
  131.2 14.5 %all_to_all.34 = f32[8,3,1536]{2,1,0:T(4,128)S(1)} all-to-all(f32[8,3,1536]{2,1,0:T(4,128)S(1)} %broadcast_in_dim.38), channel_id=1, replica_groups=mesh['group'=8,'shard_0'=4,'shard_1'=4,'shard_2'=2] {'group'}, dimensions={0} | all-to-all | bytes 294912 | tf_op jit(solution)/shard_map/all_to_all | solution.py:36
  145.7 0.1 fusion.11
  146.3 0.7 fusion.8
  (70 shorter events, 1.7 us)
Async XLA Ops:
  30.4 5.9 %copy-start.1 = (s32[1536]{0:T(1024)S(1)}, s32[1536]{0:T(1024)}, u32[]{:S(2)}) copy-start(s32[1536]{0:T(1024)} %param.7) | copy-start | bytes 18436
  31.8 20.7 %all-to-all-start.2 = ((bf16[4,32,6,1024]{3,1,2,0:T(8,128)(2,1)}), bf16[4,32,6,1024]{3,1,2,0:T(8,128)(2,1)}, u32[]{:S(2)}, u32[]{:S(2)}) async-start(bf16[4,32,6,1024]{3,1,2,0:T(8,128)(2,1)} %stack.14), calls=%async_computation.2 | async-start | bytes 3145728 | tf_op jit(solution)/shard_map/all_to_all | solution.py:22
  69.0 3.3 %copy-start = (bf16[8,4,4,2,6,1024]{5,4,3,2,1,0:T(8,128)(2,1)S(1)}, bf16[8,4,4,2,6,1024]{5,4,3,2,1,0:T(8,128)(2,1)}, u32[]{:S(2)}) copy-start(bf16[8,4,4,2,6,1024]{5,4,3,2,1,0:T(8,128)(2,1)} %gather.7) | copy-start | bytes 9437188
